TPU v7x, 32 devices: a whole 2x2x4 slice. The times are simulated.
32 devices in a mesh: gx: 8 (over y, x, core), gy: 4 (over z).
Axes of the slice: x: 2, y: 2, z: 4, core: 2. Of those that a mesh axis runs over, the one named last changes fastest.
Arguments:
- rhs_conc: float32 [16, 64, 2048], P('gx', 'gy'), may hold values from -60 to 60
- rhs_pots: float32 [16, 64, 33], P('gx', 'gy'), may hold values from -60 to 60
- diffusion: float32 [16, 64, 32], P('gx', 'gy'), may hold values from 0.05 to 5
- exchange: float32 [16, 64, 32], P('gx', 'gy'), may hold values from 0.2 to 4
- slope: float32 [16, 64, 32], P('gx', 'gy'), may hold values from 0.1 to 1
Outputs:
- sol_conc: float32 [16, 64, 2048], P('gx', 'gy')
- sol_pots: float32 [16, 64, 33], P('gx', 'gy')
All inputs are finite; a program needn't handle non-finite values.
Results may differ from a plain program's by a relative error of at most 0.0003.
Values sent between devices are 32-bit elements; how exact they have to be, the bound alone decides.
No kernel may reach another device: no remote copies, remote signals or barrier semaphores. Data moves between devices by JAX's collectives and lax.ppermute only.
A program may use at most 64 MiB of HBM per device.

v0:
```python
import jax
import jax.numpy as jnp
from jax import lax
from jax.sharding import PartitionSpec as P

ITERS = 10
node_cond = 1.0
plane_cond = 0.5
collector_cond = 2.0
epsilon = 1e-06


def padded_2(cells, sides, width):
    for axis, dim in sides:
        count = lax.axis_size(axis)
        ends = count - 1
        head = lax.slice_in_dim(cells, 0, width, axis=dim)
        tail = lax.slice_in_dim(cells, cells.shape[dim] - width, cells.shape[dim], axis=dim)
        cells = jnp.concatenate(
            [
                lax.ppermute(tail, axis, [(i, (i + 1) % count) for i in range(ends)]),
                cells,
                lax.ppermute(head, axis, [((i + 1) % count, i) for i in range(ends)]),
            ],
            axis=dim,
        )
    return cells


def mirror_laplace(values):
    inner = jnp.concatenate([values[..., :1], values[..., :-1]], axis=-1)
    outer = jnp.concatenate([values[..., 1:], values[..., -1:]], axis=-1)
    return 2.0 * values - inner - outer


def local_operator(conc, padded, diffusion, exchange, slope):
    nodes = exchange.shape[2]
    shell_count = conc.shape[2] // nodes
    shells = conc.reshape(conc.shape[0], conc.shape[1], nodes, shell_count)
    center = padded[1:-1, 1:-1]
    lateral = (
        4.0 * center - padded[2:, 1:-1] - padded[:-2, 1:-1] - padded[1:-1, 2:] - padded[1:-1, :-2]
    )
    node_pot = center[..., :nodes]
    collector = center[..., nodes]
    current = exchange * (node_pot - collector[..., None])
    surface = shells[..., shell_count - 1]
    surface_flag = (lax.broadcasted_iota(jnp.int32, (shell_count,), 0) == shell_count - 1).astype(
        jnp.float32
    )
    new_shells = (
        shells + diffusion[..., None] * mirror_laplace(shells) + current[..., None] * surface_flag
    )
    new_nodes = (
        node_cond * mirror_laplace(node_pot)
        + current
        - slope * surface
        + plane_cond * lateral[..., :nodes]
    )
    new_collector = collector_cond * lateral[..., nodes] - jnp.mean(current, axis=-1)
    return (
        new_shells.reshape(conc.shape),
        jnp.concatenate([new_nodes, new_collector[..., None]], axis=-1),
    )


def least_squares(columns, start_norm):
    count = len(columns)
    target = [start_norm] + [jnp.zeros_like(start_norm) for step in range(count)]
    cosines = []
    sines = []
    upper_rows = []
    for step in range(count):
        entries = list(columns[step])
        for row in range(step):
            first = cosines[row] * entries[row] + sines[row] * entries[row + 1]
            second = cosines[row] * entries[row + 1] - sines[row] * entries[row]
            entries[row] = first
            entries[row + 1] = second
        radius = jnp.sqrt(entries[step] * entries[step] + entries[step + 1] * entries[step + 1])
        cosine = entries[step] / radius
        sine = entries[step + 1] / radius
        entries[step] = radius
        cosines.append(cosine)
        sines.append(sine)
        lead = target[step]
        target[step] = cosine * lead
        target[step + 1] = -sine * lead
        upper_rows.append(entries[: step + 1])
    weights = [None] * count
    for row in range(count - 1, -1, -1):
        total = target[row]
        for later in range(row + 1, count):
            total = total - upper_rows[later][row] * weights[later]
        weights[row] = total / upper_rows[row][row]
    return weights


def shards(rhs_conc, rhs_pots, diffusion, exchange, slope):
    local_square = jnp.sum(rhs_conc * rhs_conc) + jnp.sum(rhs_pots * rhs_pots)
    start_norm = jnp.sqrt(lax.psum(local_square, ("gx", "gy")) + epsilon)
    basis = [(rhs_conc / start_norm, rhs_pots / start_norm)]
    columns = []
    for step in range(ITERS):
        padded = padded_2(basis[step][1], (("gx", 0), ("gy", 1)), 1)
        image_conc, image_pots = local_operator(basis[step][0], padded, diffusion, exchange, slope)
        local_dots = jnp.stack(
            [jnp.sum(vector[0] * image_conc) + jnp.sum(vector[1] * image_pots) for vector in basis]
        )
        image_square = jnp.sum(image_conc * image_conc) + jnp.sum(image_pots * image_pots)
        coeffs, total_square = lax.psum((local_dots, image_square), ("gx", "gy"))
        rest_conc, rest_pots = (image_conc, image_pots)
        for row in range(step + 1):
            rest_conc = rest_conc - coeffs[row] * basis[row][0]
            rest_pots = rest_pots - coeffs[row] * basis[row][1]
        height = jnp.sqrt(total_square - jnp.sum(coeffs * coeffs) + epsilon)
        basis.append((rest_conc / height, rest_pots / height))
        columns.append([coeffs[row] for row in range(step + 1)] + [height])
    weights = least_squares(columns, start_norm)
    sol_conc = weights[0] * basis[0][0]
    sol_pots = weights[0] * basis[0][1]
    for step in range(1, ITERS):
        sol_conc = sol_conc + weights[step] * basis[step][0]
        sol_pots = sol_pots + weights[step] * basis[step][1]
    return (sol_conc, sol_pots)


def solution(mesh):
    return jax.shard_map(
        shards,
        mesh=mesh,
        in_specs=(
            P("gx", "gy", None),
            P("gx", "gy", None),
            P("gx", "gy", None),
            P("gx", "gy", None),
            P("gx", "gy", None),
        ),
        out_specs=(P("gx", "gy", None), P("gx", "gy", None)),
        check_vma=False,
    )
```

profile of v0, /device:TPU:0, one launch (start us, length us, event | category | flops | bytes accessed | tf_op | source)
XLA Modules:
  0.0 950.6 jit_solution(5201951569017878183)
XLA Ops:
  5.1 42.0 %psum.147 = f32[]{:T(128)} all-reduce(f32[]{:T(128)S(6)} %add.632), channel_id=1, replica_groups=mesh['gx'=8,'gy'=4] {'gx','gy'}, use_global_device_ids=true, to_apply=%region_2.0 | all-reduce | flops 1 | bytes 8 | tf_op jit(solution)/shard_map/psum | solution.py:101
  57.7 4.5 collective-permute-start.3
  69.2 42.0 %all-reduce.9 = (f32[]{:T(128)}, f32[1]{0:T(128)}) all-reduce(f32[]{:T(128)S(6)} %add.639, f32[1]{0:T(128)} %bitcast.3), channel_id=1, replica_groups=mesh['gx'=8,'gy'=4] {'gx','gy'}, use_global_device_ids=true, to_apply=%region_9.0 | all-reduce | flops 2 | bytes 16 | tf_op jit(solution)/shard_map/psum | solution.py:111
  124.6 4.5 collective-permute-start.7
  137.5 42.3 %all-reduce.8 = (f32[]{:T(128)}, f32[2]{0:T(128)S(1)}) all-reduce(f32[]{:T(128)S(6)} %add.649, f32[2]{0:T(128)S(1)} %pad_maximum_fusion.120), channel_id=1, replica_groups=mesh['gx'=8,'gy'=4] {'gx','gy'}, use_global_device_ids=true, to_apply=%region_18.0 | all-reduce | flops 3 | bytes 24 | tf_op jit(solution)/shard_map/psum | solution.py:111
  196.1 4.7 collective-permute-start.11
  210.8 41.6 %all-reduce.7 = (f32[]{:T(128)}, f32[3]{0:T(128)S(1)}) all-reduce(f32[]{:T(128)S(6)} %add.660, f32[3]{0:T(128)S(1)} %pad_maximum_fusion.121), channel_id=1, replica_groups=mesh['gx'=8,'gy'=4] {'gx','gy'}, use_global_device_ids=true, to_apply=%region_30.0 | all-reduce | flops 4 | bytes 32 | tf_op jit(solution)/shard_map/psum | solution.py:111
  271.7 4.5 collective-permute-start.15
  287.7 41.9 %all-reduce.6 = (f32[]{:T(128)}, f32[4]{0:T(128)S(1)}) all-reduce(f32[]{:T(128)S(6)} %add.672, f32[4]{0:T(128)S(1)} %pad_maximum_fusion.122), channel_id=1, replica_groups=mesh['gx'=8,'gy'=4] {'gx','gy'}, use_global_device_ids=true, to_apply=%region_44.0 | all-reduce | flops 5 | bytes 40 | tf_op jit(solution)/shard_map/psum | solution.py:111
  353.1 4.5 collective-permute-start.19
  370.5 41.6 %all-reduce.5 = (f32[]{:T(128)}, f32[5]{0:T(128)S(1)}) all-reduce(f32[]{:T(128)S(6)} %add.685, f32[5]{0:T(128)S(1)} %stack.210), channel_id=1, replica_groups=mesh['gx'=8,'gy'=4] {'gx','gy'}, use_global_device_ids=true, to_apply=%region_60.0 | all-reduce | flops 6 | bytes 48 | tf_op jit(solution)/shard_map/psum | solution.py:111
  438.2 4.5 collective-permute-start.23
  456.9 41.9 %all-reduce.4 = (f32[]{:T(128)}, f32[6]{0:T(128)S(1)}) all-reduce(f32[]{:T(128)S(6)} %add.699, f32[6]{0:T(128)S(1)} %stack.217), channel_id=1, replica_groups=mesh['gx'=8,'gy'=4] {'gx','gy'}, use_global_device_ids=true, to_apply=%region_78.0 | all-reduce | flops 7 | bytes 56 | tf_op jit(solution)/shard_map/psum | solution.py:111
  530.8 4.5 collective-permute-start.27
  551.5 41.6 %all-reduce.3 = (f32[]{:T(128)}, f32[7]{0:T(128)S(1)}) all-reduce(f32[]{:T(128)S(6)} %add.714, f32[7]{0:T(128)S(1)} %stack.225), channel_id=1, replica_groups=mesh['gx'=8,'gy'=4] {'gx','gy'}, use_global_device_ids=true, to_apply=%region_98.0 | all-reduce | flops 8 | bytes 64 | tf_op jit(solution)/shard_map/psum | solution.py:111
  632.6 4.8 collective-permute-start.31
  659.6 40.8 %all-reduce.2 = (f32[]{:T(128)}, f32[8]{0:T(128)S(1)}) all-reduce(f32[]{:T(128)S(6)} %add.730, f32[8]{0:T(128)S(1)} %stack.234), channel_id=1, replica_groups=mesh['gx'=8,'gy'=4] {'gx','gy'}, use_global_device_ids=true, to_apply=%region_120.0 | all-reduce | flops 9 | bytes 72 | tf_op jit(solution)/shard_map/psum | solution.py:111
  703.1 5.0 subtract_divide_fusion.10
  710.7 5.1 subtract_divide_fusion.1
  743.7 4.5 collective-permute-start.35
  772.0 41.0 %all-reduce.1 = (f32[]{:T(128)}, f32[9]{0:T(128)S(1)}) all-reduce(f32[]{:T(128)S(6)} %add.747, f32[9]{0:T(128)S(1)} %stack.244), channel_id=1, replica_groups=mesh['gx'=8,'gy'=4] {'gx','gy'}, use_global_device_ids=true, to_apply=%region_144.0 | all-reduce | flops 10 | bytes 80 | tf_op jit(solution)/shard_map/psum | solution.py:111
  815.7 5.7 subtract_divide_fusion.9
  824.0 6.6 subtract_divide_fusion
  891.7 40.8 %all-reduce = (f32[10]{0:T(128)S(1)}, f32[]{:T(128)}) all-reduce(f32[10]{0:T(128)S(1)} %stack.255, f32[]{:T(128)S(6)} %add.765), channel_id=1, replica_groups=mesh['gx'=8,'gy'=4] {'gx','gy'}, use_global_device_ids=true, to_apply=%region_167.0 | all-reduce | flops 11 | bytes 88 | tf_op jit(solution)/shard_map/psum | solution.py:111
  (532 shorter events, 258.0 us)
Async XLA Ops:
  47.9 8.4 collective-permute-start
  49.2 7.1 collective-permute-start.1
  115.3 7.8 collective-permute-start.4
  186.2 8.4 collective-permute-start.8
  187.5 7.1 collective-permute-start.9
  260.7 9.5 collective-permute-start.12
  262.0 8.2 collective-permute-start.13
  340.0 11.7 %collective-permute-start.16 = (f32[1,16,33]{1,0,2:T(1,128)}, f32[1,16,33]{1,0,2:T(1,128)S(1)}, u32[]{:S(2)}, u32[]{:S(2)}) collective-permute-start(f32[1,16,33]{1,0,2:T(1,128)} %get-tuple-element.304), channel_id=1, source_target_pairs={{4,0},{8,4},{12,8},{16,12},{20,16},{24,20},{28,24},{5,1},{9,5},{13... | collective-permute-start | bytes 6344 | tf_op jit(solution)/shard_map/ppermute | solution.py:23
  341.3 10.4 %collective-permute-start.17 = (f32[1,16,33]{1,0,2:T(1,128)}, f32[1,16,33]{1,0,2:T(1,128)S(1)}, u32[]{:S(2)}, u32[]{:S(2)}) collective-permute-start(f32[1,16,33]{1,0,2:T(1,128)} %get-tuple-element.303), channel_id=1, source_target_pairs={{0,4},{4,8},{8,12},{12,16},{16,20},{20,24},{24,28},{1,5},{5,9},{9,... | collective-permute-start | bytes 6344 | tf_op jit(solution)/shard_map/ppermute | solution.py:21
  423.0 13.7 %collective-permute-start.20 = (f32[1,16,33]{1,0,2:T(1,128)S(1)}, f32[1,16,33]{1,0,2:T(1,128)S(1)}, u32[]{:S(2)}, u32[]{:S(2)}) collective-permute-start(f32[1,16,33]{1,0,2:T(1,128)S(1)} %get-tuple-element.297), channel_id=1, source_target_pairs={{4,0},{8,4},{12,8},{16,12},{20,16},{24,20},{28,24},{5,1},{9,5},{13... | collective-permute-start | bytes 6344 | tf_op jit(solution)/shard_map/ppermute | solution.py:23
  424.3 12.4 %collective-permute-start.21 = (f32[1,16,33]{1,0,2:T(1,128)S(1)}, f32[1,16,33]{1,0,2:T(1,128)S(1)}, u32[]{:S(2)}, u32[]{:S(2)}) collective-permute-start(f32[1,16,33]{1,0,2:T(1,128)S(1)} %get-tuple-element.296), channel_id=1, source_target_pairs={{0,4},{4,8},{8,12},{12,16},{16,20},{20,24},{24,28},{1,5},{5,9},{9,... | collective-permute-start | bytes 6344 | tf_op jit(solution)/shard_map/ppermute | solution.py:21
  514.1 15.2 %collective-permute-start.24 = (f32[1,16,33]{1,0,2:T(1,128)}, f32[1,16,33]{1,0,2:T(1,128)S(1)}, u32[]{:S(2)}, u32[]{:S(2)}) collective-permute-start(f32[1,16,33]{1,0,2:T(1,128)} %get-tuple-element.289), channel_id=1, source_target_pairs={{4,0},{8,4},{12,8},{16,12},{20,16},{24,20},{28,24},{5,1},{9,5},{13... | collective-permute-start | bytes 6344 | tf_op jit(solution)/shard_map/ppermute | solution.py:23
  515.4 13.9 %collective-permute-start.25 = (f32[1,16,33]{1,0,2:T(1,128)}, f32[1,16,33]{1,0,2:T(1,128)S(1)}, u32[]{:S(2)}, u32[]{:S(2)}) collective-permute-start(f32[1,16,33]{1,0,2:T(1,128)} %get-tuple-element.288), channel_id=1, source_target_pairs={{0,4},{4,8},{8,12},{12,16},{16,20},{20,24},{24,28},{1,5},{5,9},{9,... | collective-permute-start | bytes 6344 | tf_op jit(solution)/shard_map/ppermute | solution.py:21
  613.9 16.6 %collective-permute-start.28 = (f32[1,16,33]{1,0,2:T(1,128)}, f32[1,16,33]{1,0,2:T(1,128)S(1)}, u32[]{:S(2)}, u32[]{:S(2)}) collective-permute-start(f32[1,16,33]{1,0,2:T(1,128)} %get-tuple-element.280), channel_id=1, source_target_pairs={{4,0},{8,4},{12,8},{16,12},{20,16},{24,20},{28,24},{5,1},{9,5},{13... | collective-permute-start | bytes 6344 | tf_op jit(solution)/shard_map/ppermute | solution.py:23
  615.2 15.3 %collective-permute-start.29 = (f32[1,16,33]{1,0,2:T(1,128)}, f32[1,16,33]{1,0,2:T(1,128)}, u32[]{:S(2)}, u32[]{:S(2)}) collective-permute-start(f32[1,16,33]{1,0,2:T(1,128)} %get-tuple-element.279), channel_id=1, source_target_pairs={{0,4},{4,8},{8,12},{12,16},{16,20},{20,24},{24,28},{1,5},{5,9},{9,... | collective-permute-start | bytes 6344 | tf_op jit(solution)/shard_map/ppermute | solution.py:21
  631.3 7.2 collective-permute-start.30
  632.6 7.0 collective-permute-start.31
  725.5 16.0 %collective-permute-start.32 = (f32[1,16,33]{1,0,2:T(1,128)}, f32[1,16,33]{1,0,2:T(1,128)}, u32[]{:S(2)}, u32[]{:S(2)}) collective-permute-start(f32[1,16,33]{1,0,2:T(1,128)} %get-tuple-element.270), channel_id=1, source_target_pairs={{4,0},{8,4},{12,8},{16,12},{20,16},{24,20},{28,24},{5,1},{9,5},{13... | collective-permute-start | bytes 6344 | tf_op jit(solution)/shard_map/ppermute | solution.py:23
  726.8 14.7 %collective-permute-start.33 = (f32[1,16,33]{1,0,2:T(1,128)}, f32[1,16,33]{1,0,2:T(1,128)}, u32[]{:S(2)}, u32[]{:S(2)}) collective-permute-start(f32[1,16,33]{1,0,2:T(1,128)} %get-tuple-element.269), channel_id=1, source_target_pairs={{0,4},{4,8},{8,12},{12,16},{16,20},{20,24},{24,28},{1,5},{5,9},{9,... | collective-permute-start | bytes 6344 | tf_op jit(solution)/shard_map/ppermute | solution.py:21
  742.4 7.7 collective-permute-start.34
  841.9 17.0 %collective-permute-start.36 = (f32[1,16,33]{1,0,2:T(1,128)}, f32[1,16,33]{1,0,2:T(1,128)}, u32[]{:S(2)}, u32[]{:S(2)}) collective-permute-start(f32[1,16,33]{1,0,2:T(1,128)} %get-tuple-element.259), channel_id=1, source_target_pairs={{4,0},{8,4},{12,8},{16,12},{20,16},{24,20},{28,24},{5,1},{9,5},{13... | collective-permute-start | bytes 6344 | tf_op jit(solution)/shard_map/ppermute | solution.py:23
  843.1 15.7 %collective-permute-start.37 = (f32[1,16,33]{1,0,2:T(1,128)}, f32[1,16,33]{1,0,2:T(1,128)}, u32[]{:S(2)}, u32[]{:S(2)}) collective-permute-start(f32[1,16,33]{1,0,2:T(1,128)} %get-tuple-element.258), channel_id=1, source_target_pairs={{0,4},{4,8},{8,12},{12,16},{16,20},{20,24},{24,28},{1,5},{5,9},{9,... | collective-permute-start | bytes 6344 | tf_op jit(solution)/shard_map/ppermute | solution.py:21
  860.3 7.7 collective-permute-start.38
  861.6 7.0 collective-permute-start.39
  (79 other events, 344.7 us)
where the time goes:
time: 965 us; the launch traced here: 951 us
  blocking collectives  457 us (47%)
  between operations  171 us (18%)
  other arithmetic  118 us (12%)
  starting transfers between devices  104 us (11%)
  local copies, waits for them, and re-layouts  87.2 us (9%)
  waiting for transfers between devices  12.9 us (1%)
    psum x10, blocking collectives, shards(): coeffs, total_square = lax.psum((local_dots, image_square), ('gx', 'gy'))  415 us
    ppermute x20, starting transfers between devices, padded_2(): lax.ppermute(tail, axis, [(i, (i + 1) % count) for i in range(ends)])  78.2 us
    div x18, other arithmetic, shards(): basis.append((rest_conc / height, rest_pots / height))  58.3 us
    psum x1, blocking collectives, shards(): start_norm = jnp.sqrt(lax.psum(local_square, ('gx', 'gy')) + epsilon)  42 us
    ppermute x20, starting transfers between devices, padded_2(): lax.ppermute(head, axis, [((i + 1) % count, i) for i in range(ends)])  25.8 us
  transfers between devices with their start and end apart: 40, of which 10 were waited for; matrix products, arithmetic and copies ran while one was open for 4% of the time, Pallas kernels for 0%

commit v1 on v0

--- a/solution.py
+++ b/solution.py
@@ -108,7 +108,7 @@
             [jnp.sum(vector[0] * image_conc) + jnp.sum(vector[1] * image_pots) for vector in basis]
         )
         image_square = jnp.sum(image_conc * image_conc) + jnp.sum(image_pots * image_pots)
-        coeffs, total_square = lax.psum((local_dots, image_square), ("gx", "gy"))
+        coeffs, total_square = lax.psum(lax.psum((local_dots, image_square), "gy"), "gx")
         rest_conc, rest_pots = (image_conc, image_pots)
         for row in range(step + 1):
             rest_conc = rest_conc - coeffs[row] * basis[row][0]

time: 965 us -> 791 us (0.82)
  blocking collectives: 457 us -> 282 us
    psum x10 -> x20, blocking collectives: 415 us -> 240 us  [the longest x10 125 us: shards(): lax.psum(lax.psum((local_dots, image_square), 'gy'), 'gx')]
  transfers between devices with their start and end apart: 40 -> 40, of which waited for: 10 -> 15; matrix products, arithmetic and copies ran while one was open for 4% -> 5% of each run, Pallas kernels for 0% -> 0%
where the time goes in v1:
time: 791 us; the launch traced here: 776 us
  blocking collectives  282 us (36%)
  between operations  171 us (22%)
  other arithmetic  118 us (15%)
  starting transfers between devices  104 us (13%)
  local copies, waits for them, and re-layouts  87.2 us (11%)
  waiting for transfers between devices  14.5 us (2%)
    psum x10, blocking collectives, shards(): lax.psum(lax.psum((local_dots, image_square), 'gy'), 'gx')  125 us
    psum x10, blocking collectives, shards(): lax.psum((local_dots, image_square), 'gy')  115 us
    ppermute x20, starting transfers between devices, padded_2(): lax.ppermute(tail, axis, [(i, (i + 1) % count) for i in range(ends)])  77.8 us
    div x18, other arithmetic, shards(): basis.append((rest_conc / height, rest_pots / height))  58.3 us
    psum x1, blocking collectives, shards(): start_norm = jnp.sqrt(lax.psum(local_square, ('gx', 'gy')) + epsilon)  42 us
    ppermute x20, starting transfers between devices, padded_2(): lax.ppermute(head, axis, [((i + 1) % count, i) for i in range(ends)])  25.8 us
    unnamed x139, local copies, waits for them, and re-layouts  18.5 us
  transfers between devices with their start and end apart: 40, of which 15 were waited for; matrix products, arithmetic and copies ran while one was open for 5% of the time, Pallas kernels for 0%

profile of v1, /device:TPU:0, one launch (start us, length us, event | category | flops | bytes accessed | tf_op | source)
XLA Modules:
  0.0 776.1 jit_solution(11603291778760787407)
XLA Ops:
  5.1 42.0 %psum.287 = f32[]{:T(128)} all-reduce(f32[]{:T(128)S(6)} %add.672), channel_id=1, replica_groups=mesh['gx'=8,'gy'=4] {'gx','gy'}, use_global_device_ids=true, to_apply=%region_2.0 | all-reduce | flops 1 | bytes 8 | tf_op jit(solution)/shard_map/psum | solution.py:101
  69.2 13.7 %all-reduce.19 = (f32[]{:T(128)}, f32[1]{0:T(128)}) all-reduce(f32[]{:T(128)S(6)} %add.679, f32[1]{0:T(128)} %bitcast.3), channel_id=1, replica_groups=mesh['gx'=8,'gy'=4] {'gy'}, use_global_device_ids=true, to_apply=%region_10.0 | all-reduce | flops 2 | bytes 16 | tf_op jit(solution)/shard_map/psum | solution.py:111
  82.9 12.4 %all-reduce.9 = (f32[]{:T(128)}, f32[1]{0:T(128)}) all-reduce(f32[]{:T(128)} %get-tuple-element.177, f32[1]{0:T(128)} %get-tuple-element.178), channel_id=1, replica_groups=mesh['gx'=8,'gy'=4] {'gx'}, use_global_device_ids=true, to_apply=%region_11.0 | all-reduce | flops 2 | bytes 16 | tf_op jit(solution)/shard_map/psum | solution.py:111
  122.0 11.4 %all-reduce.18 = (f32[]{:T(128)}, f32[2]{0:T(128)S(1)}) all-reduce(f32[]{:T(128)S(6)} %add.689, f32[2]{0:T(128)S(1)} %pad_maximum_fusion.120), channel_id=1, replica_groups=mesh['gx'=8,'gy'=4] {'gy'}, use_global_device_ids=true, to_apply=%region_21.0 | all-reduce | flops 3 | bytes 24 | tf_op jit(solution)/shard_map/psum | solution.py:111
  133.4 12.4 %all-reduce.8 = (f32[]{:T(128)}, f32[2]{0:T(128)S(1)}) all-reduce(f32[]{:T(128)} %get-tuple-element.175, f32[2]{0:T(128)S(1)} %get-tuple-element.176), channel_id=1, replica_groups=mesh['gx'=8,'gy'=4] {'gx'}, use_global_device_ids=true, to_apply=%region_22.0 | all-reduce | flops 3 | bytes 24 | tf_op jit(solution)/shard_map/psum | solution.py:111
  177.2 11.3 %all-reduce.17 = (f32[]{:T(128)}, f32[3]{0:T(128)S(1)}) all-reduce(f32[]{:T(128)S(6)} %add.700, f32[3]{0:T(128)S(1)} %pad_maximum_fusion.121), channel_id=1, replica_groups=mesh['gx'=8,'gy'=4] {'gy'}, use_global_device_ids=true, to_apply=%region_35.0 | all-reduce | flops 4 | bytes 32 | tf_op jit(solution)/shard_map/psum | solution.py:111
  188.6 12.9 %all-reduce.7 = (f32[]{:T(128)}, f32[3]{0:T(128)S(1)}) all-reduce(f32[]{:T(128)} %get-tuple-element.173, f32[3]{0:T(128)S(1)} %get-tuple-element.174), channel_id=1, replica_groups=mesh['gx'=8,'gy'=4] {'gx'}, use_global_device_ids=true, to_apply=%region_36.0 | all-reduce | flops 4 | bytes 32 | tf_op jit(solution)/shard_map/psum | solution.py:111
  237.2 11.3 %all-reduce.16 = (f32[]{:T(128)}, f32[4]{0:T(128)S(1)}) all-reduce(f32[]{:T(128)S(6)} %add.712, f32[4]{0:T(128)S(1)} %pad_maximum_fusion.122), channel_id=1, replica_groups=mesh['gx'=8,'gy'=4] {'gy'}, use_global_device_ids=true, to_apply=%region_51.0 | all-reduce | flops 5 | bytes 40 | tf_op jit(solution)/shard_map/psum | solution.py:111
  248.5 12.4 %all-reduce.6 = (f32[]{:T(128)}, f32[4]{0:T(128)S(1)}) all-reduce(f32[]{:T(128)} %get-tuple-element.171, f32[4]{0:T(128)S(1)} %get-tuple-element.172), channel_id=1, replica_groups=mesh['gx'=8,'gy'=4] {'gx'}, use_global_device_ids=true, to_apply=%region_52.0 | all-reduce | flops 5 | bytes 40 | tf_op jit(solution)/shard_map/psum | solution.py:111
  302.4 11.3 %all-reduce.15 = (f32[]{:T(128)}, f32[5]{0:T(128)S(1)}) all-reduce(f32[]{:T(128)S(6)} %add.725, f32[5]{0:T(128)S(1)} %stack.210), channel_id=1, replica_groups=mesh['gx'=8,'gy'=4] {'gy'}, use_global_device_ids=true, to_apply=%region_69.0 | all-reduce | flops 6 | bytes 48 | tf_op jit(solution)/shard_map/psum | solution.py:111
  313.7 12.4 %all-reduce.5 = (f32[]{:T(128)}, f32[5]{0:T(128)S(1)}) all-reduce(f32[]{:T(128)} %get-tuple-element.169, f32[5]{0:T(128)S(1)} %get-tuple-element.170), channel_id=1, replica_groups=mesh['gx'=8,'gy'=4] {'gx'}, use_global_device_ids=true, to_apply=%region_70.0 | all-reduce | flops 6 | bytes 48 | tf_op jit(solution)/shard_map/psum | solution.py:111
  371.1 11.3 %all-reduce.14 = (f32[]{:T(128)}, f32[6]{0:T(128)S(1)}) all-reduce(f32[]{:T(128)S(6)} %add.739, f32[6]{0:T(128)S(1)} %stack.217), channel_id=1, replica_groups=mesh['gx'=8,'gy'=4] {'gy'}, use_global_device_ids=true, to_apply=%region_89.0 | all-reduce | flops 7 | bytes 56 | tf_op jit(solution)/shard_map/psum | solution.py:111
  382.4 12.6 %all-reduce.4 = (f32[]{:T(128)}, f32[6]{0:T(128)S(1)}) all-reduce(f32[]{:T(128)} %get-tuple-element.167, f32[6]{0:T(128)S(1)} %get-tuple-element.168), channel_id=1, replica_groups=mesh['gx'=8,'gy'=4] {'gx'}, use_global_device_ids=true, to_apply=%region_90.0 | all-reduce | flops 7 | bytes 56 | tf_op jit(solution)/shard_map/psum | solution.py:111
  448.3 11.3 %all-reduce.13 = (f32[]{:T(128)}, f32[7]{0:T(128)S(1)}) all-reduce(f32[]{:T(128)S(6)} %add.754, f32[7]{0:T(128)S(1)} %stack.225), channel_id=1, replica_groups=mesh['gx'=8,'gy'=4] {'gy'}, use_global_device_ids=true, to_apply=%region_111.0 | all-reduce | flops 8 | bytes 64 | tf_op jit(solution)/shard_map/psum | solution.py:111
  459.6 12.4 %all-reduce.3 = (f32[]{:T(128)}, f32[7]{0:T(128)S(1)}) all-reduce(f32[]{:T(128)} %get-tuple-element.165, f32[7]{0:T(128)S(1)} %get-tuple-element.166), channel_id=1, replica_groups=mesh['gx'=8,'gy'=4] {'gx'}, use_global_device_ids=true, to_apply=%region_112.0 | all-reduce | flops 8 | bytes 64 | tf_op jit(solution)/shard_map/psum | solution.py:111
  538.0 11.2 %all-reduce.12 = (f32[]{:T(128)}, f32[8]{0:T(128)S(1)}) all-reduce(f32[]{:T(128)S(6)} %add.770, f32[8]{0:T(128)S(1)} %stack.234), channel_id=1, replica_groups=mesh['gx'=8,'gy'=4] {'gy'}, use_global_device_ids=true, to_apply=%region_135.0 | all-reduce | flops 9 | bytes 72 | tf_op jit(solution)/shard_map/psum | solution.py:111
  549.2 12.4 %all-reduce.2 = (f32[]{:T(128)}, f32[8]{0:T(128)S(1)}) all-reduce(f32[]{:T(128)} %get-tuple-element.163, f32[8]{0:T(128)S(1)} %get-tuple-element.164), channel_id=1, replica_groups=mesh['gx'=8,'gy'=4] {'gx'}, use_global_device_ids=true, to_apply=%region_136.0 | all-reduce | flops 9 | bytes 72 | tf_op jit(solution)/shard_map/psum | solution.py:111
  572.0 5.1 subtract_divide_fusion.1
  632.9 11.1 %all-reduce.11 = (f32[]{:T(128)}, f32[9]{0:T(128)S(1)}) all-reduce(f32[]{:T(128)S(6)} %add.787, f32[9]{0:T(128)S(1)} %stack.244), channel_id=1, replica_groups=mesh['gx'=8,'gy'=4] {'gy'}, use_global_device_ids=true, to_apply=%region_161.0 | all-reduce | flops 10 | bytes 80 | tf_op jit(solution)/shard_map/psum | solution.py:111
  644.0 12.4 %all-reduce.1 = (f32[]{:T(128)}, f32[9]{0:T(128)S(1)}) all-reduce(f32[]{:T(128)} %get-tuple-element.161, f32[9]{0:T(128)S(1)} %get-tuple-element.162), channel_id=1, replica_groups=mesh['gx'=8,'gy'=4] {'gx'}, use_global_device_ids=true, to_apply=%region_162.0 | all-reduce | flops 10 | bytes 80 | tf_op jit(solution)/shard_map/psum | solution.py:111
  659.0 5.7 subtract_divide_fusion.9
  667.3 6.6 subtract_divide_fusion
  734.5 11.2 %all-reduce.10 = (f32[10]{0:T(128)S(1)}, f32[]{:T(128)}) all-reduce(f32[10]{0:T(128)S(1)} %stack.255, f32[]{:T(128)S(6)} %add.805), channel_id=1, replica_groups=mesh['gx'=8,'gy'=4] {'gy'}, use_global_device_ids=true, to_apply=%region_185.0 | all-reduce | flops 11 | bytes 88 | tf_op jit(solution)/shard_map/psum | solution.py:111
  745.7 12.4 %all-reduce = (f32[10]{0:T(128)S(1)}, f32[]{:T(128)}) all-reduce(f32[10]{0:T(128)S(1)} %get-tuple-element.159, f32[]{:T(128)} %get-tuple-element.160), channel_id=1, replica_groups=mesh['gx'=8,'gy'=4] {'gx'}, use_global_device_ids=true, to_apply=%region_186.0 | all-reduce | flops 11 | bytes 88 | tf_op jit(solution)/shard_map/psum | solution.py:111
  (542 shorter events, 305.5 us)
Async XLA Ops:
  47.9 8.4 %collective-permute-start = (f32[1,16,33]{1,0,2:T(1,128)S(1)}, f32[1,16,33]{1,0,2:T(1,128)S(1)}, u32[]{:S(2)}, u32[]{:S(2)}) collective-permute-start(f32[1,16,33]{1,0,2:T(1,128)S(1)} %get-tuple-element.352), channel_id=1, source_target_pairs={{4,0},{8,4},{12,8},{16,12},{20,16},{24,20},{28,24},{5,1},{9,5},{13... | collective-permute-start | bytes 6344 | tf_op jit(solution)/shard_map/ppermute | solution.py:23
  49.2 7.1 collective-permute-start.1
  99.4 7.8 collective-permute-start.4
  108.6 6.9 collective-permute-start.7
  152.2 8.4 %collective-permute-start.8 = (f32[1,16,33]{1,0,2:T(1,128)S(1)}, f32[1,16,33]{1,0,2:T(1,128)S(1)}, u32[]{:S(2)}, u32[]{:S(2)}) collective-permute-start(f32[1,16,33]{1,0,2:T(1,128)S(1)} %get-tuple-element.338), channel_id=1, source_target_pairs={{4,0},{8,4},{12,8},{16,12},{20,16},{24,20},{28,24},{5,1},{9,5},{13... | collective-permute-start | bytes 6344 | tf_op jit(solution)/shard_map/ppermute | solution.py:23
  153.5 7.1 collective-permute-start.9
  162.0 6.9 collective-permute-start.11
  209.7 9.5 %collective-permute-start.12 = (f32[1,16,33]{1,0,2:T(1,128)S(1)}, f32[1,16,33]{1,0,2:T(1,128)S(1)}, u32[]{:S(2)}, u32[]{:S(2)}) collective-permute-start(f32[1,16,33]{1,0,2:T(1,128)S(1)} %get-tuple-element.331), channel_id=1, source_target_pairs={{4,0},{8,4},{12,8},{16,12},{20,16},{24,20},{28,24},{5,1},{9,5},{13... | collective-permute-start | bytes 6344 | tf_op jit(solution)/shard_map/ppermute | solution.py:23
  211.0 8.2 %collective-permute-start.13 = (f32[1,16,33]{1,0,2:T(1,128)S(1)}, f32[1,16,33]{1,0,2:T(1,128)S(1)}, u32[]{:S(2)}, u32[]{:S(2)}) collective-permute-start(f32[1,16,33]{1,0,2:T(1,128)S(1)} %get-tuple-element.330), channel_id=1, source_target_pairs={{0,4},{4,8},{8,12},{12,16},{16,20},{20,24},{24,28},{1,5},{5,9},{9,... | collective-permute-start | bytes 6344 | tf_op jit(solution)/shard_map/ppermute | solution.py:21
  271.3 11.7 %collective-permute-start.16 = (f32[1,16,33]{1,0,2:T(1,128)}, f32[1,16,33]{1,0,2:T(1,128)S(1)}, u32[]{:S(2)}, u32[]{:S(2)}) collective-permute-start(f32[1,16,33]{1,0,2:T(1,128)} %get-tuple-element.324), channel_id=1, source_target_pairs={{4,0},{8,4},{12,8},{16,12},{20,16},{24,20},{28,24},{5,1},{9,5},{13... | collective-permute-start | bytes 6344 | tf_op jit(solution)/shard_map/ppermute | solution.py:23
  272.6 10.4 %collective-permute-start.17 = (f32[1,16,33]{1,0,2:T(1,128)}, f32[1,16,33]{1,0,2:T(1,128)S(1)}, u32[]{:S(2)}, u32[]{:S(2)}) collective-permute-start(f32[1,16,33]{1,0,2:T(1,128)} %get-tuple-element.323), channel_id=1, source_target_pairs={{0,4},{4,8},{8,12},{12,16},{16,20},{20,24},{24,28},{1,5},{5,9},{9,... | collective-permute-start | bytes 6344 | tf_op jit(solution)/shard_map/ppermute | solution.py:21
  337.0 13.5 %collective-permute-start.20 = (f32[1,16,33]{1,0,2:T(1,128)S(1)}, f32[1,16,33]{1,0,2:T(1,128)S(1)}, u32[]{:S(2)}, u32[]{:S(2)}) collective-permute-start(f32[1,16,33]{1,0,2:T(1,128)S(1)} %get-tuple-element.317), channel_id=1, source_target_pairs={{4,0},{8,4},{12,8},{16,12},{20,16},{24,20},{28,24},{5,1},{9,5},{13... | collective-permute-start | bytes 6344 | tf_op jit(solution)/shard_map/ppermute | solution.py:23
  338.3 12.2 %collective-permute-start.21 = (f32[1,16,33]{1,0,2:T(1,128)S(1)}, f32[1,16,33]{1,0,2:T(1,128)S(1)}, u32[]{:S(2)}, u32[]{:S(2)}) collective-permute-start(f32[1,16,33]{1,0,2:T(1,128)S(1)} %get-tuple-element.316), channel_id=1, source_target_pairs={{0,4},{4,8},{8,12},{12,16},{16,20},{20,24},{24,28},{1,5},{5,9},{9,... | collective-permute-start | bytes 6344 | tf_op jit(solution)/shard_map/ppermute | solution.py:21
  410.4 15.2 %collective-permute-start.24 = (f32[1,16,33]{1,0,2:T(1,128)}, f32[1,16,33]{1,0,2:T(1,128)S(1)}, u32[]{:S(2)}, u32[]{:S(2)}) collective-permute-start(f32[1,16,33]{1,0,2:T(1,128)} %get-tuple-element.309), channel_id=1, source_target_pairs={{4,0},{8,4},{12,8},{16,12},{20,16},{24,20},{28,24},{5,1},{9,5},{13... | collective-permute-start | bytes 6344 | tf_op jit(solution)/shard_map/ppermute | solution.py:23
  411.7 13.9 %collective-permute-start.25 = (f32[1,16,33]{1,0,2:T(1,128)}, f32[1,16,33]{1,0,2:T(1,128)S(1)}, u32[]{:S(2)}, u32[]{:S(2)}) collective-permute-start(f32[1,16,33]{1,0,2:T(1,128)} %get-tuple-element.308), channel_id=1, source_target_pairs={{0,4},{4,8},{8,12},{12,16},{16,20},{20,24},{24,28},{1,5},{5,9},{9,... | collective-permute-start | bytes 6344 | tf_op jit(solution)/shard_map/ppermute | solution.py:21
  492.8 16.6 %collective-permute-start.28 = (f32[1,16,33]{1,0,2:T(1,128)}, f32[1,16,33]{1,0,2:T(1,128)S(1)}, u32[]{:S(2)}, u32[]{:S(2)}) collective-permute-start(f32[1,16,33]{1,0,2:T(1,128)} %get-tuple-element.300), channel_id=1, source_target_pairs={{4,0},{8,4},{12,8},{16,12},{20,16},{24,20},{28,24},{5,1},{9,5},{13... | collective-permute-start | bytes 6344 | tf_op jit(solution)/shard_map/ppermute | solution.py:23
  494.1 15.3 %collective-permute-start.29 = (f32[1,16,33]{1,0,2:T(1,128)}, f32[1,16,33]{1,0,2:T(1,128)}, u32[]{:S(2)}, u32[]{:S(2)}) collective-permute-start(f32[1,16,33]{1,0,2:T(1,128)} %get-tuple-element.299), channel_id=1, source_target_pairs={{0,4},{4,8},{8,12},{12,16},{16,20},{20,24},{24,28},{1,5},{5,9},{9,... | collective-permute-start | bytes 6344 | tf_op jit(solution)/shard_map/ppermute | solution.py:21
  510.3 7.0 collective-permute-start.30
  586.7 16.0 %collective-permute-start.32 = (f32[1,16,33]{1,0,2:T(1,128)}, f32[1,16,33]{1,0,2:T(1,128)}, u32[]{:S(2)}, u32[]{:S(2)}) collective-permute-start(f32[1,16,33]{1,0,2:T(1,128)} %get-tuple-element.290), channel_id=1, source_target_pairs={{4,0},{8,4},{12,8},{16,12},{20,16},{24,20},{28,24},{5,1},{9,5},{13... | collective-permute-start | bytes 6344 | tf_op jit(solution)/shard_map/ppermute | solution.py:23
  588.0 14.7 %collective-permute-start.33 = (f32[1,16,33]{1,0,2:T(1,128)}, f32[1,16,33]{1,0,2:T(1,128)}, u32[]{:S(2)}, u32[]{:S(2)}) collective-permute-start(f32[1,16,33]{1,0,2:T(1,128)} %get-tuple-element.289), channel_id=1, source_target_pairs={{0,4},{4,8},{8,12},{12,16},{16,20},{20,24},{24,28},{1,5},{5,9},{9,... | collective-permute-start | bytes 6344 | tf_op jit(solution)/shard_map/ppermute | solution.py:21
  603.6 7.9 %collective-permute-start.34 = (f32[4,1,33]{1,0,2:T(4,128)S(1)}, f32[4,1,33]{1,0,2:T(4,128)S(1)}, u32[]{:S(2)}, u32[]{:S(2)}) collective-permute-start(f32[4,1,33]{1,0,2:T(4,128)S(1)} %get-tuple-element.250), channel_id=1, source_target_pairs={{1,0},{2,1},{3,2},{5,4},{6,5},{7,6},{9,8},{10,9},{11,10},{13,12},{... | collective-permute-start | bytes 1592 | tf_op jit(solution)/shard_map/ppermute | solution.py:23
  685.2 17.0 %collective-permute-start.36 = (f32[1,16,33]{1,0,2:T(1,128)}, f32[1,16,33]{1,0,2:T(1,128)}, u32[]{:S(2)}, u32[]{:S(2)}) collective-permute-start(f32[1,16,33]{1,0,2:T(1,128)} %get-tuple-element.279), channel_id=1, source_target_pairs={{4,0},{8,4},{12,8},{16,12},{20,16},{24,20},{28,24},{5,1},{9,5},{13... | collective-permute-start | bytes 6344 | tf_op jit(solution)/shard_map/ppermute | solution.py:23
  686.5 15.7 %collective-permute-start.37 = (f32[1,16,33]{1,0,2:T(1,128)}, f32[1,16,33]{1,0,2:T(1,128)}, u32[]{:S(2)}, u32[]{:S(2)}) collective-permute-start(f32[1,16,33]{1,0,2:T(1,128)} %get-tuple-element.278), channel_id=1, source_target_pairs={{0,4},{4,8},{8,12},{12,16},{16,20},{20,24},{24,28},{1,5},{5,9},{9,... | collective-permute-start | bytes 6344 | tf_op jit(solution)/shard_map/ppermute | solution.py:21
  703.6 7.7 collective-permute-start.38
  (79 other events, 331.1 us)
